TPU v7x, 32 devices: a whole 2x2x4 slice. The times are simulated.
32 devices in a mesh: gx: 8 (over y, x, core), gz: 4 (over z).
Axes of the slice: x: 2, y: 2, z: 4, core: 2. Of those that a mesh axis runs over, the one named last changes fastest.
Arguments:
- velocity: float32 [3, 64, 64, 512], P(None, 'gx', None, 'gz'), may hold values from -40 to 40
Outputs:
- coefficient: float32 [64], replicated
- eddy_viscosity: float32 [64, 64, 512], P('gx', None, 'gz')
All inputs are finite; a program needn't handle non-finite values.
Results may differ from a plain program's by a relative error of at most 0.0001.
Values sent between devices are 32-bit elements; how exact they have to be, the bound alone decides.
A program may use at most 64 MiB of HBM per device.

v0:
```python
import functools

import jax
import jax.numpy as jnp
from jax import lax
from jax.experimental import pallas as pl
from jax.experimental.pallas import tpu as pltpu
from jax.sharding import PartitionSpec as P

pairs = ((0, 0), (1, 1), (2, 2), (0, 1), (0, 2), (1, 2))
PAD = 8
MESH = pl.DeviceIdType.MESH
EARLY_A = False


def shear_terms(dx, dy, dz):
    terms = (dx[0], dy[1], dz[2], dx[1] + dy[0], dx[2] + dz[0], dy[2] + dz[1])
    square = [term * term for term in terms]
    total = 0.5 * (square[0] + square[1] + square[2]) + 0.25 * (square[3] + square[4] + square[5])
    return terms, jnp.sqrt(total)


def contraction(leonard, model):
    numer = leonard[0] * model[0]
    for slot in range(1, 6):
        numer = numer + leonard[slot] * model[slot]
    square = [term * term for term in model]
    denom = (square[0] + square[1] + square[2]) + 0.5 * (square[3] + square[4] + square[5])
    return numer, denom


def kernel(
    axes, sizes, vel, sums_out, mag_out,
    U, HU, ST, MAG, ACC, LO, HI, RLO, RHI, BACK, GOT,
    load_sem, send_sem, recv_sem, sum_send, sum_recv,
):
    nx, nz = sizes
    count = nx * nz
    gx, gz = lax.axis_index(axes[0]), lax.axis_index(axes[1])
    X, Y, Z = vel.shape[1:]
    xl, xr = lax.rem(gx + nx - 1, nx), lax.rem(gx + 1, nx)
    zl, zr = lax.rem(gz + nz - 1, nz), lax.rem(gz + 1, nz)
    rows = pl.ds(PAD, Y)
    me = gx * nz + gz

    load = pltpu.make_async_copy(vel, U.at[:, pl.ds(2, X), rows, :], load_sem)
    load.start()

    def to_all(body):
        def step(k, carry):
            body((lax.rem(gx + k // nz, nx), lax.rem(gz + lax.rem(k, nz), nz)))
            return carry

        lax.fori_loop(1, count, step, 0, unroll=min(count - 1, 31))

    barrier = pltpu.get_barrier_semaphore()
    to_all(lambda peer: pl.semaphore_signal(barrier, inc=1, device_id=peer, device_id_type=MESH))

    def send(slot, src, dst, peer):
        copy = pltpu.make_async_remote_copy(
            src_ref=src, dst_ref=dst, send_sem=send_sem.at[slot], recv_sem=recv_sem.at[slot],
            device_id=peer, device_id_type=MESH,
        )
        copy.start()
        return copy

    load.wait()

    lane = lax.broadcasted_iota(jnp.int32, (Y, Z), 1)
    span = 4 * X
    for c in range(3):
        tile = jnp.zeros((Y, Z), jnp.float32)
        for x in range(X):
            plane = U[c, x + 2, PAD:PAD + Y, :]
            top = pltpu.roll(plane, (4 + 4 * x) % Z, 1)
            bottom = pltpu.roll(plane, span + 4 * x, 1)
            tile = jnp.where((lane >= 4 * x) & (lane < 4 * x + 4), top, tile)
            tile = jnp.where((lane >= span + 4 * x) & (lane < span + 4 * x + 4), bottom, tile)
        turned = jnp.concatenate([tile, tile], axis=0).T
        for t in range(X // 2):
            LO[c, t + 1] = turned[8 * t:8 * t + 8, :]
            HI[c, t + 1] = turned[span + 8 * t:span + 8 * t + 8, :]

    def ghosts(ref, first, count):
        span = pl.ds(first, count)
        ref[:, span, PAD - 1:PAD, :] = (
            2.0 * ref[:, span, PAD:PAD + 1, :] - ref[:, span, PAD + 1:PAD + 2, :]
        )
        end = PAD + Y
        ref[:, span, end:end + 1, :] = (
            2.0 * ref[:, span, end - 1:end, :] - ref[:, span, end - 2:end - 1, :]
        )

    def z_sum(f):
        pair = f + pltpu.roll(f, 1, 1)
        return pair + pltpu.roll(pair, Z - 1, 1)

    def z_diff(f):
        return pltpu.roll(f, Z - 1, 1) - pltpu.roll(f, 1, 1)

    def stage_a(p):
        for r in range(PAD, PAD + Y, 8):
            u = [U[i, p, r:r + 8, :] for i in range(3)]
            up = [U[i, p + 1, r:r + 8, :] for i in range(3)]
            um = [U[i, p - 1, r:r + 8, :] for i in range(3)]
            dx = [up[i] - um[i] for i in range(3)]
            dy = [U[i, p, r + 1:r + 9, :] - U[i, p, r - 1:r + 7, :] for i in range(3)]
            dz = [z_diff(u[i]) for i in range(3)]
            terms, mag = shear_terms(dx, dy, dz)
            MAG[p, r - PAD:r - PAD + 8, :] = mag
            for slot in range(6):
                ST[slot, p, r - PAD:r - PAD + 8, :] = mag * terms[slot]
            for i in range(3):
                HU[i, p, r:r + 8, :] = 0.25 * z_sum((up[i] + um[i]) + 2.0 * u[i])
        ghosts(HU, p, 1)

    inner = lax.broadcasted_iota(jnp.int32, (8, Z), 1)
    inner = (inner >= 2) & (inner < Z - 2)

    def stage_b(p):
        for r in range(PAD, PAD + Y, 8):
            q = slice(r - PAD, r - PAD + 8)
            h = [HU[i, p, r:r + 8, :] for i in range(3)]
            dx = [HU[i, p + 1, r:r + 8, :] - HU[i, p - 1, r:r + 8, :] for i in range(3)]
            dy = [HU[i, p, r + 1:r + 9, :] - HU[i, p, r - 1:r + 7, :] for i in range(3)]
            dz = [z_diff(h[i]) for i in range(3)]
            terms, mag = shear_terms(dx, dy, dz)
            mag = 4.0 * mag
            u = [[U[i, p + k, r:r + 8, :] for i in range(3)] for k in (-1, 0, 1)]
            leonard, model = [], []
            for slot, (i, j) in enumerate(pairs):
                prod = (u[0][i] * u[0][j] + u[2][i] * u[2][j]) + 2.0 * (u[1][i] * u[1][j])
                leonard.append(z_sum(prod) - h[i] * h[j])
                stress = (ST[slot, p - 1, q, :] + ST[slot, p + 1, q, :]) + 2.0 * ST[slot, p, q, :]
                model.append(z_sum(stress) - mag * terms[slot])
            numer, denom = contraction(leonard, model)
            ACC[q, :] += jnp.where(inner, numer, 0.0)
            ACC[r - PAD + Y:r - PAD + Y + 8, :] += jnp.where(inner, denom, 0.0)

    def each(first, last, body):
        def step(p, carry):
            body(p)
            return carry

        lax.fori_loop(first, last, step, 0)

    ACC[...] = jnp.zeros_like(ACC)
    ghosts(U, 2, X)
    if EARLY_A:
        each(3, X + 1, stage_a)
    pl.semaphore_wait(barrier, count - 1)

    half = X // 2
    mid, low, high = pl.ds(1, half), pl.ds(1, 1), pl.ds(half, 1)
    before, after = pl.ds(0, 1), pl.ds(half + 1, 1)
    edges = [
        send(0, LO.at[:, low], RLO.at[:, after], (xl, zr)),
        send(1, LO.at[:, high], RLO.at[:, before], (xr, zr)),
        send(2, HI.at[:, low], RHI.at[:, after], (xl, zl)),
        send(3, HI.at[:, high], RHI.at[:, before], (xr, zl)),
        send(4, LO.at[:, mid], RLO.at[:, mid], (gx, zr)),
        send(5, HI.at[:, mid], RHI.at[:, mid], (gx, zl)),
        send(6, LO.at[:, low], LO.at[:, after], (xl, gz)),
        send(7, LO.at[:, high], LO.at[:, before], (xr, gz)),
        send(8, HI.at[:, low], HI.at[:, after], (xl, gz)),
        send(9, HI.at[:, high], HI.at[:, before], (xr, gz)),
    ]

    def send_plane(slot, x, ext, peer):
        return send(slot, vel.at[:, pl.ds(x, 1)], U.at[:, pl.ds(ext, 1), rows, :], peer)

    near = [send_plane(10, 0, X + 2, (xl, gz)), send_plane(11, X - 1, 1, (xr, gz))]
    far = [send_plane(12, 1, X + 3, (xl, gz)), send_plane(13, X - 2, 0, (xr, gz))]

    if not EARLY_A:
        each(3, X + 1, stage_a)
    each(4, X, stage_b)

    for copy in near:
        copy.wait_recv()
    ghosts(U, 1, 1)
    ghosts(U, X + 2, 1)
    each(0, 2, lambda s: stage_a(2 + s * (X - 1)))
    each(0, 2, lambda s: stage_b(3 + s * (X - 3)))
    for copy in edges:
        copy.wait_recv()
    W = X + 4
    ln = lax.broadcasted_iota(jnp.int32, (W, 8, 2 * Y), 2)
    sub = lax.broadcasted_iota(jnp.int32, (W, 8, 2 * Y), 1)
    left = ln < Y

    def y_diff(f, n):
        y = ln[:n] - jnp.where(left[:n], 0, Y)
        plus, minus = pltpu.roll(f, 2 * Y - 1, 2), pltpu.roll(f, 1, 2)
        return jnp.where(y == Y - 1, 2.0 * f, jnp.where(y == 0, 2.0 * plus, plus)) - jnp.where(
            y == 0, 2.0 * f, jnp.where(y == Y - 1, 2.0 * minus, minus)
        )

    def s_diff(f):
        return pltpu.roll(f, 7, 1) - pltpu.roll(f, 1, 1)

    def s_sum(f):
        pair = f + pltpu.roll(f, 1, 1)
        return pair + pltpu.roll(pair, 7, 1)

    def x_sum(f):
        return (f[:-2] + f[2:]) + 2.0 * f[1:-1]

    w = []
    head = sub[:2] < 4
    for c in range(3):
        found = []
        for t in range(W // 2):
            upper = jnp.where(left[0], RLO[c, t], LO[c, t])
            lower = jnp.where(left[0], HI[c, t], RHI[c, t])
            found.append(jnp.where(head[0], upper, pltpu.roll(lower, 4, 0)))
            found.append(jnp.where(head[0], pltpu.roll(upper, 4, 0), lower))
        w.append(jnp.stack(found))
    terms, wmag = shear_terms(
        [f[2:] - f[:-2] for f in w],
        [y_diff(f[1:-1], W - 2) for f in w],
        [s_diff(f[1:-1]) for f in w],
    )
    hw = [0.25 * s_sum(x_sum(f)) for f in w]
    test, tmag = shear_terms(
        [f[2:] - f[:-2] for f in hw],
        [y_diff(f[1:-1], X) for f in hw],
        [s_diff(f[1:-1]) for f in hw],
    )
    tmag = 4.0 * tmag
    leonard, model = [], []
    for slot, (i, j) in enumerate(pairs):
        prod = w[i][1:-1] * w[j][1:-1]
        leonard.append(s_sum(x_sum(prod)) - hw[i][1:-1] * hw[j][1:-1])
        model.append(s_sum(x_sum(wmag * terms[slot])) - tmag * test[slot])
    numer, denom = contraction(leonard, model)
    numer, denom = jnp.sum(numer, axis=0), jnp.sum(denom, axis=0)
    s2, l2 = sub[0], left[0]
    take = (l2 & ((s2 == 4) | (s2 == 5))) | (~l2 & ((s2 == 2) | (s2 == 3)))
    numer = jnp.sum(jnp.where(take, numer, 0.0), axis=0, keepdims=True)
    denom = jnp.sum(jnp.where(take, denom, 0.0), axis=0, keepdims=True)
    numer = numer + pltpu.roll(numer, Y, 1)
    denom = denom + pltpu.roll(denom, Y, 1)
    window_sums = jnp.where(l2[:1], numer, denom)

    back = wmag[1:-1].reshape(8 * X, 2 * Y)
    back = jnp.concatenate([back, jnp.zeros((Z - 8 * X, 2 * Y), jnp.float32)], axis=0).T
    BACK[...] = back

    for copy in far:
        copy.wait_recv()
    ghosts(U, 0, 1)
    ghosts(U, X + 3, 1)
    each(0, 2, lambda s: stage_a(1 + s * (X + 1)))
    each(0, 2, lambda s: stage_b(2 + s * (X - 1)))

    GOT[me] = window_sums + jnp.sum(ACC[...].T, axis=0, keepdims=True)

    def total_copy(peer):
        return pltpu.make_async_remote_copy(
            src_ref=GOT.at[me], dst_ref=GOT.at[me], send_sem=sum_send, recv_sem=sum_recv,
            device_id=peer, device_id_type=MESH,
        )

    to_all(lambda peer: total_copy(peer).start())
    for x in range(X):
        low_lane = pltpu.roll(BACK[:Y], (Z - 8 * x - 4) % Z, 1)
        high_lane = pltpu.roll(BACK[Y:], (Z - 1 - 8 * x - 3) % Z, 1)
        mag = MAG[x + 2]
        mag_out[x] = jnp.where(lane == 0, low_lane, jnp.where(lane == Z - 1, high_lane, mag))
    for copy in edges + near + far:
        copy.wait_send()
    everyone = GOT.at[pl.ds(0, count - 1)]
    pltpu.make_async_copy(everyone, everyone, sum_recv).wait()
    sums_out[...] = jnp.sum(GOT[...], axis=0)
    pltpu.make_async_copy(everyone, everyone, sum_send).wait()


def finish(cells, sums, mag, coef_out, visc_out):
    X, Y, Z = mag.shape
    total = sums[...] * (1.0 / (256.0 * cells))
    coef = total / (pltpu.roll(total, Y, 1) + 1e-6)
    coef_out[...] = coef[0, :Y]
    wide = jnp.broadcast_to(coef, (Z, 2 * Y)).T[:Y]
    for x in range(X):
        visc_out[x] = wide * mag[x]


def on_device(axes, sizes, velocity):
    X, Y, Z = velocity.shape[1:]
    nx, nz = sizes
    f32 = jnp.float32
    tall = Y + 2 * PAD
    W = X + 4
    dma = pltpu.SemaphoreType.DMA
    cells = X * nx * Z * nz
    vmem = pl.BlockSpec(memory_space=pltpu.VMEM)
    strip = pltpu.VMEM((3, W // 2, 8, 2 * Y), f32)
    sums, mag = pl.pallas_call(
        functools.partial(kernel, axes, sizes),
        out_shape=(pltpu.VMEM((1, 2 * Y), f32), pltpu.VMEM((X, Y, Z), f32)),
        in_specs=[pl.BlockSpec(memory_space=pl.ANY)],
        out_specs=(vmem, vmem),
        scratch_shapes=[
            pltpu.VMEM((3, W, tall, Z), f32),
            pltpu.VMEM((3, W, tall, Z), f32),
            pltpu.VMEM((6, W, Y, Z), f32),
            pltpu.VMEM((W, Y, Z), f32),
            pltpu.VMEM((2 * Y, Z), f32),
            strip,
            strip,
            strip,
            strip,
            pltpu.VMEM((2 * Y, Z), f32),
            pltpu.VMEM((nx * nz, 1, 2 * Y), f32),
            dma,
            dma((14,)),
            dma((14,)),
            dma,
            dma,
        ],
        compiler_params=pltpu.CompilerParams(collective_id=0, has_side_effects=True),
    )(velocity)
    return pl.pallas_call(
        functools.partial(finish, cells),
        out_shape=(jax.ShapeDtypeStruct((Y,), f32), jax.ShapeDtypeStruct((X, Y, Z), f32)),
        in_specs=[vmem, vmem],
        out_specs=(vmem, vmem),
    )(*(pltpu.with_memory_space_constraint(a, pltpu.VMEM) for a in (sums, mag)))


def solution(mesh):
    axes = ("gx", "gz")
    sizes = tuple(mesh.shape[axis] for axis in axes)
    return jax.shard_map(
        functools.partial(on_device, axes, sizes),
        mesh=mesh,
        in_specs=(P(None, "gx", None, "gz"),),
        out_specs=(P(), P("gx", None, "gz")),
        check_vma=False,
    )
```

profile of v0, /device:TPU:0, one launch (start us, length us, event | category | flops | bytes accessed | tf_op | source)
XLA Modules:
  0.0 20.6 jit_solution(11395693726139251640)
XLA Ops:
  0.6 19.1 %shard_map.30 = (f32[1,128]{1,0:T(1,128)S(1)}, f32[8,64,128]{2,1,0:T(8,128)S(1)}) custom-call(f32[3,8,64,128]{3,2,1,0:T(8,128)} %vel.1), custom_call_target="tpu_custom_call" | custom-call | tf_op jit(solution)/shard_map/pallas_call | solution.py:299
  19.7 0.9 %shard_map.31 = (f32[64]{0:T(128)}, f32[8,64,128]{2,1,0:T(8,128)}) custom-call(f32[1,128]{1,0:T(1,128)S(1)} %get-tuple-element.4.sums, f32[8,64,128]{2,1,0:T(8,128)S(1)} %get-tuple-element.5.mag), custom_call_target="tpu_custom_call" | custom-call | tf_op jit(solution)/shard_map/pallas_call | solution.py:324
where the time goes:
time: 20.8 us; the launch traced here: 20.6 us
  Pallas kernels  20 us (96%)
  between operations  0.64 us (3%)
    pallas_call x1, Pallas kernels, on_device(): pl.pallas_call(functools.partial(kernel, axes, sizes), out_shape=(pltpu.V...  19.1 us
    pallas_call x1, Pallas kernels, on_device(): pl.pallas_call(functools.partial(finish, cells), out_shape=(jax.ShapeDtyp...  0.87 us

commit v1 on v0

v1 whole, which is shorter than its diff:
```python
import functools

import jax
import jax.numpy as jnp
from jax import lax
from jax.experimental import pallas as pl
from jax.experimental.pallas import tpu as pltpu
from jax.sharding import PartitionSpec as P

pairs = ((0, 0), (1, 1), (2, 2), (0, 1), (0, 2), (1, 2))
PAD = 8
TINY = 1.1754943508222875e-38
MESH = pl.DeviceIdType.MESH


def shear_terms(dx, dy, dz, scale):
    terms = (dx[0], dy[1], dz[2], dx[1] + dy[0], dx[2] + dz[0], dy[2] + dz[1])
    square = [term * term for term in terms]
    total = (0.5 * scale) * (square[0] + square[1] + square[2]) + (0.25 * scale) * (
        square[3] + square[4] + square[5]
    )
    return terms, total * lax.rsqrt(jnp.maximum(total, TINY))


def z_parts(u, plus, minus):
    twice = [f + f for f in u]
    zs = [(plus[i] + minus[i]) + twice[i] for i in range(3)]
    dz = [plus[i] - minus[i] for i in range(3)]
    pz = [(plus[i] * plus[j] + minus[i] * minus[j]) + twice[i] * u[j] for i, j in pairs]
    return zs, dz, pz


def contraction(leonard, model):
    numer = leonard[0] * model[0]
    for slot in range(1, 6):
        numer = numer + leonard[slot] * model[slot]
    square = [term * term for term in model]
    denom = (square[0] + square[1] + square[2]) + 0.5 * (square[3] + square[4] + square[5])
    return numer, denom


def kernel(
    axes, sizes, vel, sums_out, mag_out,
    U, ZS, DZ, PZ, HU, ST, MAG, ACC,
    ZT, ZB, RT, RB, EX, GX, GL, GR, WZ, WP, WS, WH, WM, WD, BACK, GOT,
    load_sem, send_sem, recv_sem, sum_send, sum_recv, row_sem,
):
    nx, nz = sizes
    count = nx * nz
    gx, gz = lax.axis_index(axes[0]), lax.axis_index(axes[1])
    X, Y, Z = vel.shape[1:]
    W = X + 4
    half = X // 2
    xl, xr = lax.rem(gx + nx - 1, nx), lax.rem(gx + 1, nx)
    zl, zr = lax.rem(gz + nz - 1, nz), lax.rem(gz + 1, nz)
    rows = pl.ds(PAD, Y)
    me = gx * nz + gz

    load = pltpu.make_async_copy(vel, U.at[:, pl.ds(2, X), rows, :], load_sem)
    load.start()

    def to_line(body, size, peer):
        def step(k, carry):
            body(peer(k))
            return carry

        lax.fori_loop(1, size, step, 0, unroll=min(size - 1, 31))

    def in_row(k):
        return (lax.rem(gx + k, nx), gz)

    def in_column(k):
        return (gx, lax.rem(gz + k, nz))

    def anywhere(k):
        return (lax.rem(gx + k // nz, nx), lax.rem(gz + lax.rem(k, nz), nz))

    def signal(sem):
        return lambda peer: pl.semaphore_signal(sem, inc=1, device_id=peer, device_id_type=MESH)

    barrier = pltpu.get_barrier_semaphore()
    to_line(signal(barrier), nz, in_column)
    to_line(signal(barrier), nx, in_row)

    def send(slot, src, dst, peer):
        copy = pltpu.make_async_remote_copy(
            src_ref=src, dst_ref=dst, send_sem=send_sem.at[slot], recv_sem=recv_sem.at[slot],
            device_id=peer, device_id_type=MESH,
        )
        copy.start()
        return copy

    def send_plane(slot, x, ext, peer):
        src = U.at[:, pl.ds(x + 2, 1), rows, :]
        return send(slot, src, U.at[:, pl.ds(ext, 1), rows, :], peer)

    load.wait()

    tile = (8, 2 * Y)
    sub = lax.broadcasted_iota(jnp.int32, tile, 0)
    lane = lax.broadcasted_iota(jnp.int32, tile, 1)
    top, left = sub < 4, lane < Y

    def swap(f):
        return pltpu.roll(f, Y, 1)

    def turn(f):
        return pltpu.roll(f, 4, 0)

    for c in range(3):
        low, high = [], []
        for k in range(half):
            both = [U[c, 2 + k + side * half, PAD:PAD + Y, :] for side in range(2)]
            turned = jnp.concatenate(both, axis=0).T
            low.append(turned[:8])
            high.append(turned[Z - 8:])
        for j in range(half // 2):
            ZT[c, j] = jnp.where(top, turn(high[2 * j]), high[2 * j + 1])
            ZB[c, j] = jnp.where(top, low[2 * j], turn(low[2 * j + 1]))
        last = half // 2 - 1
        EX[0, c] = jnp.where(left, ZT[c, 0], swap(ZB[c, 0]))
        EX[1, c] = jnp.where(left, swap(ZT[c, last]), ZB[c, last])

    pl.semaphore_wait(barrier, nx + nz - 2)
    beside = [send(0, EX.at[0], GX.at[1], (xl, gz)), send(1, EX.at[1], GX.at[0], (xr, gz))]
    edges = [send(2, ZT, RT, (gx, zr)), send(3, ZB, RB, (gx, zl))]
    near = [send_plane(4, 0, X + 2, (xl, gz)), send_plane(5, X - 1, 1, (xr, gz))]
    far = [send_plane(6, 1, X + 3, (xl, gz)), send_plane(7, X - 2, 0, (xr, gz))]
    to_line(signal(row_sem), nx, in_row)

    def ghosts(ref, planes):
        end = PAD + Y
        for p in planes:
            for c in range(3):
                ref[c, p, PAD - 1:PAD, :] = (
                    2.0 * ref[c, p, PAD:PAD + 1, :] - ref[c, p, PAD + 1:PAD + 2, :]
                )
                ref[c, p, end:end + 1, :] = (
                    2.0 * ref[c, p, end - 1:end, :] - ref[c, p, end - 2:end - 1, :]
                )

    def ahead(f):
        return pltpu.roll(f, Z - 1, 1)

    def behind(f):
        return pltpu.roll(f, 1, 1)

    kept = {2: 0, X + 1: 1, 1: 2, X + 2: 3}

    def along_z(p, r, slope):
        q = slice(r, r + 8)
        u = [U[i, p, PAD + r:PAD + r + 8, :] for i in range(3)]
        zs, dz, pz = z_parts(u, [ahead(f) for f in u], [behind(f) for f in u])
        for i in range(3):
            ZS[i, p, q, :] = zs[i]
        if 1 <= p <= X + 2:
            for slot in range(6):
                PZ[slot, p, q, :] = pz[slot]
        if p in kept:
            for i in range(3):
                DZ[i, kept[p], q, :] = dz[i]
        slope[p] = dz

    def rates(p, r, slope):
        q = slice(r, r + 8)
        m = PAD + r
        dx = [U[i, p + 1, m:m + 8, :] - U[i, p - 1, m:m + 8, :] for i in range(3)]
        dy = [U[i, p, m + 1:m + 9, :] - U[i, p, m - 1:m + 7, :] for i in range(3)]
        dz = slope[p] if p in slope else [DZ[i, kept[p], q, :] for i in range(3)]
        terms, mag = shear_terms(dx, dy, dz, 1.0)
        MAG[p, q, :] = mag
        for slot in range(6):
            ST[slot, p, q, :] = mag * terms[slot]

    def smooth(planes, r):
        q = slice(r, r + 8)
        for i in range(3):
            pair = {}
            for p in planes:
                for s in (p - 1, p):
                    if s not in pair:
                        pair[s] = ZS[i, s, q, :] + ZS[i, s + 1, q, :]
                HU[i, p, PAD + r:PAD + r + 8, :] = 0.25 * (pair[p - 1] + pair[p])

    def stage_a(z_planes, planes):
        for r in range(0, Y, 8):
            slope = {}
            for p in z_planes:
                along_z(p, r, slope)
            for p in planes:
                rates(p, r, slope)
            smooth(planes, r)
        ghosts(HU, planes)

    def test_side(h, dx, dy, dz, px, sz):
        terms, mag = shear_terms(dx, dy, dz, 16.0)
        leonard = [px[slot] - h[i] * h[j] for slot, (i, j) in enumerate(pairs)]
        model = [sz[slot] - mag * terms[slot] for slot in range(6)]
        return contraction(leonard, model)

    def stage_b(planes):
        for r in range(0, Y, 8):
            q = slice(r, r + 8)
            m = PAD + r
            pair = {}

            def x_sum(ref, slot, p):
                for s in (p - 1, p):
                    if (id(ref), slot, s) not in pair:
                        pair[id(ref), slot, s] = ref[slot, s, q, :] + ref[slot, s + 1, q, :]
                return pair[id(ref), slot, p - 1] + pair[id(ref), slot, p]

            total = None
            for p in planes:
                h = [HU[i, p, m:m + 8, :] for i in range(3)]
                dx = [HU[i, p + 1, m:m + 8, :] - HU[i, p - 1, m:m + 8, :] for i in range(3)]
                dy = [HU[i, p, m + 1:m + 9, :] - HU[i, p, m - 1:m + 7, :] for i in range(3)]
                dz = [ahead(f) - behind(f) for f in h]
                px = [x_sum(PZ, slot, p) for slot in range(6)]
                sz = []
                for slot in range(6):
                    sx = x_sum(ST, slot, p)
                    two = sx + behind(sx)
                    sz.append(two + ahead(two))
                found = test_side(h, dx, dy, dz, px, sz)
                total = found if total is None else [a + b for a, b in zip(total, found)]
            ACC[q, :] += total[0]
            ACC[r + Y:r + Y + 8, :] += total[1]

    ACC[...] = jnp.zeros_like(ACC)
    WD[...] = jnp.zeros_like(WD)
    own = range(2, X + 2)
    ghosts(U, own)
    stage_a(own, range(3, X + 1))
    stage_b(range(4, X))

    for copy in beside:
        copy.wait_recv()
    corners = [send(8, GX, GL, (gx, zr)), send(9, GX, GR, (gx, zl))]

    for copy in near:
        copy.wait_recv()
    ghosts(U, (1, X + 2))
    stage_a((1, X + 2), (2, X + 1))
    stage_b((3,))
    stage_b((X,))

    y = lane - jnp.where(left, 0, Y)
    plus_by = jnp.where(y == 0, 2.0, jnp.where(y == Y - 1, 0.0, 1.0))
    minus_by = jnp.where(y == 0, 0.0, jnp.where(y == Y - 1, 2.0, 1.0))
    self_by = jnp.where(y == 0, -2.0, jnp.where(y == Y - 1, 2.0, 0.0))

    def y_diff(f):
        plus, minus = pltpu.roll(f, 2 * Y - 1, 1), pltpu.roll(f, 1, 1)
        return (plus_by * plus - minus_by * minus) + self_by * f

    def up(f):
        return pltpu.roll(f, 7, 0)

    def down(f):
        return pltpu.roll(f, 1, 0)

    def join(odd, first, second):
        return jnp.where(top, turn(first) if odd else first, second if odd else turn(second))

    def window_a(cells, planes):
        slope = {}
        for p in cells:
            u = cells[p]
            zs, dz, pz = z_parts(u, [up(f) for f in u], [down(f) for f in u])
            for i in range(3):
                WZ[i, p] = zs[i]
                WZ[3 + i, p] = u[i]
                WZ[6 + i, p] = dz[i]
            for slot in range(6):
                WP[slot, p] = pz[slot]
        for p in planes:
            dx = [WZ[3 + i, p + 1] - WZ[3 + i, p - 1] for i in range(3)]
            dy = [y_diff(WZ[3 + i, p]) for i in range(3)]
            dz = [WZ[6 + i, p] for i in range(3)]
            terms, mag = shear_terms(dx, dy, dz, 1.0)
            WM[p] = mag
            for slot in range(6):
                WS[slot, p] = mag * terms[slot]
            for i in range(3):
                WH[i, p] = 0.25 * ((WZ[i, p - 1] + WZ[i, p]) + (WZ[i, p] + WZ[i, p + 1]))

    def window_b(planes):
        total = None
        for p in planes:
            h = [WH[i, p] for i in range(3)]
            dx = [WH[i, p + 1] - WH[i, p - 1] for i in range(3)]
            dy = [y_diff(f) for f in h]
            dz = [up(f) - down(f) for f in h]
            px = [(WP[s, p - 1] + WP[s, p]) + (WP[s, p] + WP[s, p + 1]) for s in range(6)]
            sz = []
            for s in range(6):
                two = (WS[s, p - 1] + WS[s, p]) + (WS[s, p] + WS[s, p + 1])
                two = two + down(two)
                sz.append(two + up(two))
            found = test_side(h, dx, dy, dz, px, sz)
            total = found if total is None else [a + b for a, b in zip(total, found)]
        WD[0] += total[0]
        WD[1] += total[1]

    for copy in edges:
        copy.wait_recv()
    cells = {p: [] for p in own}
    for c in range(3):
        for j in range(half // 2):
            rt, zt, zb, rb = RT[c, j], ZT[c, j], ZB[c, j], RB[c, j]
            first = (jnp.where(left, rt, swap(zt)), jnp.where(left, swap(rt), zt))
            second = (jnp.where(left, zb, swap(rb)), jnp.where(left, swap(zb), rb))
            for odd in range(2):
                for side in range(2):
                    cells[2 + 2 * j + odd + side * half].append(join(odd, first[side], second[side]))
    window_a(cells, range(3, X + 1))
    window_b(range(4, X))

    for copy in far:
        copy.wait_recv()
    ghosts(U, (0, X + 3))
    stage_a((0, X + 3), (1, X + 2))
    stage_b((2,))
    stage_b((X + 1,))

    for copy in corners:
        copy.wait_recv()
    cells = {0: [], 1: [], X + 2: [], X + 3: []}
    for c in range(3):
        for side in range(2):
            mine, lower, upper = swap(GX[side, c]), GL[side, c], GR[side, c]
            first, second = jnp.where(left, lower, mine), jnp.where(left, mine, upper)
            for odd in range(2):
                cells[side * (X + 2) + odd].append(join(odd, first, second))
    window_a(cells, (1, 2, X + 1, X + 2))
    window_b((2, 3, X, X + 1))

    take = (left & ((sub == 4) | (sub == 5))) | (~left & ((sub == 2) | (sub == 3)))
    numer = jnp.sum(jnp.where(take, WD[0], 0.0), axis=0, keepdims=True)
    denom = jnp.sum(jnp.where(take, WD[1], 0.0), axis=0, keepdims=True)
    numer = numer + swap(numer)
    denom = denom + swap(denom)
    window_sums = jnp.where(left[:1], numer, denom)
    turned = jnp.sum(ACC[...].T[2:Z - 2], axis=0, keepdims=True)
    GOT[me] = window_sums + turned

    def total_copy(peer):
        return pltpu.make_async_remote_copy(
            src_ref=GOT.at[me], dst_ref=GOT.at[me], send_sem=sum_send, recv_sem=sum_recv,
            device_id=peer, device_id_type=MESH,
        )

    pl.semaphore_wait(row_sem, nx - 1)
    to_line(lambda peer: total_copy(peer).start(), count, anywhere)

    back = jnp.concatenate([WM[p] for p in own], axis=0)
    back = jnp.concatenate([back, jnp.zeros((Z - 8 * X, 2 * Y), jnp.float32)], axis=0).T
    BACK[...] = back
    spot = lax.broadcasted_iota(jnp.int32, (Y, Z), 1)
    for x in range(X):
        low_lane = pltpu.roll(BACK[:Y], (Z - 8 * x - 4) % Z, 1)
        high_lane = pltpu.roll(BACK[Y:], (Z - 1 - 8 * x - 3) % Z, 1)
        mag = MAG[x + 2]
        mag_out[x] = jnp.where(spot == 0, low_lane, jnp.where(spot == Z - 1, high_lane, mag))
    for copy in beside + edges + near + far + corners:
        copy.wait_send()
    everyone = GOT.at[pl.ds(0, count - 1)]
    pltpu.make_async_copy(everyone, everyone, sum_recv).wait()
    sums_out[...] = jnp.sum(GOT[...], axis=0)
    pltpu.make_async_copy(everyone, everyone, sum_send).wait()


def finish(cells, sums, mag, coef_out, visc_out):
    X, Y, Z = mag.shape
    total = sums[...] * (1.0 / (256.0 * cells))
    coef = total / (pltpu.roll(total, Y, 1) + 1e-6)
    coef_out[...] = coef[0, :Y]
    wide = jnp.broadcast_to(coef, (Z, 2 * Y)).T[:Y]
    for x in range(X):
        visc_out[x] = wide * mag[x]


def on_device(axes, sizes, velocity):
    X, Y, Z = velocity.shape[1:]
    nx, nz = sizes
    f32 = jnp.float32
    tall = Y + 2 * PAD
    W = X + 4
    dma = pltpu.SemaphoreType.DMA
    cells = X * nx * Z * nz
    vmem = pl.BlockSpec(memory_space=pltpu.VMEM)
    strip = pltpu.VMEM((3, X // 4, 8, 2 * Y), f32)
    ends = pltpu.VMEM((2, 3, 8, 2 * Y), f32)
    sums, mag = pl.pallas_call(
        functools.partial(kernel, axes, sizes),
        out_shape=(pltpu.VMEM((1, 2 * Y), f32), pltpu.VMEM((X, Y, Z), f32)),
        in_specs=[pl.BlockSpec(memory_space=pl.ANY)],
        out_specs=(vmem, vmem),
        scratch_shapes=[
            pltpu.VMEM((3, W, tall, Z), f32),
            pltpu.VMEM((3, W, Y, Z), f32),
            pltpu.VMEM((3, 4, Y, Z), f32),
            pltpu.VMEM((6, W, Y, Z), f32),
            pltpu.VMEM((3, W, tall, Z), f32),
            pltpu.VMEM((6, W, Y, Z), f32),
            pltpu.VMEM((W, Y, Z), f32),
            pltpu.VMEM((2 * Y, Z), f32),
            strip,
            strip,
            strip,
            strip,
            ends,
            ends,
            ends,
            ends,
            pltpu.VMEM((9, W, 8, 2 * Y), f32),
            pltpu.VMEM((6, W, 8, 2 * Y), f32),
            pltpu.VMEM((6, W, 8, 2 * Y), f32),
            pltpu.VMEM((3, W, 8, 2 * Y), f32),
            pltpu.VMEM((W, 8, 2 * Y), f32),
            pltpu.VMEM((2, 8, 2 * Y), f32),
            pltpu.VMEM((2 * Y, Z), f32),
            pltpu.VMEM((nx * nz, 1, 2 * Y), f32),
            dma,
            dma((10,)),
            dma((10,)),
            dma,
            dma,
            pltpu.SemaphoreType.REGULAR,
        ],
        compiler_params=pltpu.CompilerParams(collective_id=0, has_side_effects=True),
    )(velocity)
    return pl.pallas_call(
        functools.partial(finish, cells),
        out_shape=(jax.ShapeDtypeStruct((Y,), f32), jax.ShapeDtypeStruct((X, Y, Z), f32)),
        in_specs=[vmem, vmem],
        out_specs=(vmem, vmem),
    )(*(pltpu.with_memory_space_constraint(a, pltpu.VMEM) for a in (sums, mag)))


def solution(mesh):
    axes = ("gx", "gz")
    sizes = tuple(mesh.shape[axis] for axis in axes)
    return jax.shard_map(
        functools.partial(on_device, axes, sizes),
        mesh=mesh,
        in_specs=(P(None, "gx", None, "gz"),),
        out_specs=(P(), P("gx", None, "gz")),
        check_vma=False,
    )
```

time: 20.8 us -> 18.9 us (0.909)
  Pallas kernels: 20 us -> 18.1 us
    pallas_call x1, Pallas kernels: 19.1 us -> 17.3 us  [on_device(): pl.pallas_call(functools.partial(kernel, axes, sizes), out_shape=(pltpu.V...]
where the time goes in v1:
time: 18.9 us; the launch traced here: 18.8 us
  Pallas kernels  18.1 us (96%)
  between operations  0.64 us (3%)
    pallas_call x1, Pallas kernels, on_device(): pl.pallas_call(functools.partial(kernel, axes, sizes), out_shape=(pltpu.V...  17.3 us
    pallas_call x1, Pallas kernels, on_device(): pl.pallas_call(functools.partial(finish, cells), out_shape=(jax.ShapeDtyp...  0.87 us

profile of v1, /device:TPU:0, one launch (start us, length us, event | category | flops | bytes accessed | tf_op | source)
XLA Modules:
  0.0 18.8 jit_solution(1190567379528507340)
XLA Ops:
  0.6 17.3 %shard_map.30 = (f32[1,128]{1,0:T(1,128)S(1)}, f32[8,64,128]{2,1,0:T(8,128)S(1)}) custom-call(f32[3,8,64,128]{3,2,1,0:T(8,128)} %vel.1), custom_call_target="tpu_custom_call" | custom-call | tf_op jit(solution)/shard_map/pallas_call | solution.py:395
  17.9 0.9 %shard_map.31 = (f32[64]{0:T(128)}, f32[8,64,128]{2,1,0:T(8,128)}) custom-call(f32[1,128]{1,0:T(1,128)S(1)} %get-tuple-element.4.sums, f32[8,64,128]{2,1,0:T(8,128)S(1)} %get-tuple-element.5.mag), custom_call_target="tpu_custom_call" | custom-call | tf_op jit(solution)/shard_map/pallas_call | solution.py:434

commit v2 on v1

--- a/solution.py
+++ b/solution.py
@@ -39,11 +39,20 @@
     return numer, denom
 
 
+def knowledge_rounds(size):
+    reach, columns, rounds = 1, 0, []
+    while reach < size // 2 or columns < size // 2:
+        step = min(reach, 2 * columns + 1, size // 2 - columns)
+        rounds.append(step)
+        reach, columns = reach + step, columns + step
+    return rounds
+
+
 def kernel(
     axes, sizes, vel, sums_out, mag_out,
     U, ZS, DZ, PZ, HU, ST, MAG, ACC,
     ZT, ZB, RT, RB, EX, GX, GL, GR, WZ, WP, WS, WH, WM, WD, BACK, GOT,
-    load_sem, send_sem, recv_sem, sum_send, sum_recv, row_sem,
+    load_sem, send_sem, recv_sem, sum_send, sum_recv, row_sem, wrap_sem, all_sem,
 ):
     nx, nz = sizes
     count = nx * nz
@@ -56,8 +65,14 @@
     rows = pl.ds(PAD, Y)
     me = gx * nz + gz
 
-    load = pltpu.make_async_copy(vel, U.at[:, pl.ds(2, X), rows, :], load_sem)
-    load.start()
+    loads = [
+        pltpu.make_async_copy(
+            vel.at[:, pl.ds(x, size)], U.at[:, pl.ds(x + 2, size), rows, :], load_sem.at[slot]
+        )
+        for slot, (x, size) in enumerate(((0, 2), (X - 2, 2), (2, X - 4)))
+    ]
+    for load in loads:
+        load.start()
 
     def to_line(body, size, peer):
         def step(k, carry):
@@ -66,35 +81,45 @@
 
         lax.fori_loop(1, size, step, 0, unroll=min(size - 1, 31))
 
-    def in_row(k):
-        return (lax.rem(gx + k, nx), gz)
-
-    def in_column(k):
-        return (gx, lax.rem(gz + k, nz))
-
     def anywhere(k):
-        return (lax.rem(gx + k // nz, nx), lax.rem(gz + lax.rem(k, nz), nz))
+        spot = gz * nx + gx
+        peer = k - 1 + jnp.where(k > spot, 1, 0)
+        return (lax.rem(peer, nx), peer // nx)
 
     def signal(sem):
         return lambda peer: pl.semaphore_signal(sem, inc=1, device_id=peer, device_id_type=MESH)
 
     barrier = pltpu.get_barrier_semaphore()
-    to_line(signal(barrier), nz, in_column)
-    to_line(signal(barrier), nx, in_row)
+    for peer in ((xl, gz), (xr, gz)):
+        signal(barrier)(peer)
+
+    def to_column(sem, distance):
+        @pl.when((gz + distance >= 0) & (gz + distance < nz))
+        def _():
+            signal(sem)((gx, gz + distance))
+
+    to_column(barrier, -1)
+    for distance in range(1, nz):
+        to_column(barrier, distance)
 
     def send(slot, src, dst, peer):
         copy = pltpu.make_async_remote_copy(
             src_ref=src, dst_ref=dst, send_sem=send_sem.at[slot], recv_sem=recv_sem.at[slot],
             device_id=peer, device_id_type=MESH,
         )
-        copy.start()
         return copy
 
-    def send_plane(slot, x, ext, peer):
-        src = U.at[:, pl.ds(x + 2, 1), rows, :]
-        return send(slot, src, U.at[:, pl.ds(ext, 1), rows, :], peer)
-
-    load.wait()
+    deep = Y // 2
+    parts = ((0, Y, 1), (0, deep, 0), (deep, deep, 0))
+
+    def halo_copy(part, side, ext, dst, peer):
+        first, size, _ = parts[part]
+        span = pl.ds(PAD + first, size)
+        slot = 4 + 2 * part + side
+        return pltpu.make_async_remote_copy(
+            src_ref=U.at[:, pl.ds(ext, 1), span, :], dst_ref=U.at[:, pl.ds(dst, 1), span, :],
+            send_sem=send_sem.at[slot], recv_sem=recv_sem.at[slot], device_id=peer, device_id_type=MESH,
+        )
 
     tile = (8, 2 * Y)
     sub = lax.broadcasted_iota(jnp.int32, tile, 0)
@@ -107,26 +132,70 @@
     def turn(f):
         return pltpu.roll(f, 4, 0)
 
-    for c in range(3):
-        low, high = [], []
-        for k in range(half):
-            both = [U[c, 2 + k + side * half, PAD:PAD + Y, :] for side in range(2)]
-            turned = jnp.concatenate(both, axis=0).T
-            low.append(turned[:8])
-            high.append(turned[Z - 8:])
-        for j in range(half // 2):
-            ZT[c, j] = jnp.where(top, turn(high[2 * j]), high[2 * j + 1])
-            ZB[c, j] = jnp.where(top, low[2 * j], turn(low[2 * j + 1]))
-        last = half // 2 - 1
-        EX[0, c] = jnp.where(left, ZT[c, 0], swap(ZB[c, 0]))
-        EX[1, c] = jnp.where(left, swap(ZT[c, last]), ZB[c, last])
-
-    pl.semaphore_wait(barrier, nx + nz - 2)
-    beside = [send(0, EX.at[0], GX.at[1], (xl, gz)), send(1, EX.at[1], GX.at[0], (xr, gz))]
+    def partner(k):
+        return X - 2 + k if k < 2 else half + k - 2
+
+    def strips(j):
+        for c in range(3):
+            low, high = [], []
+            for k in (2 * j, 2 * j + 1):
+                both = [U[c, 2 + x, PAD:PAD + Y, :] for x in (k, partner(k))]
+                turned = jnp.concatenate(both, axis=0).T
+                low.append(turned[:8])
+                high.append(turned[Z - 8:])
+            tops = jnp.where(top, turn(high[0]), high[1])
+            bottoms = jnp.where(top, low[0], turn(low[1]))
+            ZT[c, j] = tops
+            ZB[c, j] = bottoms
+            if j == 0:
+                EX[0, c] = jnp.where(left, tops, swap(bottoms))
+                EX[1, c] = jnp.where(left, swap(tops), bottoms)
+
+    rounds = knowledge_rounds(nx)
+
+    def tell(turn):
+        for peer in sorted({rounds[turn] % nx, -rounds[turn] % nx}):
+            signal(row_sem.at[turn])((lax.rem(gx + peer, nx), gz))
+
+    def spread(turns):
+        @pl.when(gz == nz - 1)
+        def _():
+            for k in turns:
+                pl.semaphore_wait(row_sem.at[k], len({rounds[k] % nx, -rounds[k] % nx}))
+                if k + 1 < len(rounds):
+                    tell(k + 1)
+                else:
+                    for z in range(nz - 1):
+                        signal(all_sem)((gx, z))
+
+    pl.semaphore_wait(barrier, 2 + gz + jnp.where(gz < nz - 1, 1, 0))
+
+    @pl.when(gz == nz - 1)
+    def _():
+        signal(wrap_sem)((gx, 0))
+        tell(0)
+
+    loads[0].wait()
+    loads[1].wait()
+    strips(0)
+    beside = [send(0, EX.at[1], GX.at[0], (xr, gz)), send(1, EX.at[0], GX.at[1], (xl, gz))]
+    for copy in beside:
+        copy.start()
     edges = [send(2, ZT, RT, (gx, zr)), send(3, ZB, RB, (gx, zl))]
-    near = [send_plane(4, 0, X + 2, (xl, gz)), send_plane(5, X - 1, 1, (xr, gz))]
-    far = [send_plane(6, 1, X + 3, (xl, gz)), send_plane(7, X - 2, 0, (xr, gz))]
-    to_line(signal(row_sem), nx, in_row)
+    halo = []
+    for part, (_, _, ext) in enumerate(parts):
+        halo.append(halo_copy(part, 0, X + ext, ext, (xr, gz)))
+        halo.append(halo_copy(part, 1, 3 - ext, X + 3 - ext, (xl, gz)))
+    for copy in halo:
+        copy.start()
+    loads[2].wait()
+    for j in range(1, half // 2):
+        strips(j)
+    edges[0].start()
+
+    @pl.when(gz > 0)
+    def _():
+        edges[1].start()
 
     def ghosts(ref, planes):
         end = PAD + Y
@@ -145,34 +214,41 @@
     def behind(f):
         return pltpu.roll(f, 1, 1)
 
-    kept = {2: 0, X + 1: 1, 1: 2, X + 2: 3}
-
-    def along_z(p, r, slope):
+    def along_z(p, r, slope, keep, partial):
         q = slice(r, r + 8)
         u = [U[i, p, PAD + r:PAD + r + 8, :] for i in range(3)]
         zs, dz, pz = z_parts(u, [ahead(f) for f in u], [behind(f) for f in u])
         for i in range(3):
             ZS[i, p, q, :] = zs[i]
-        if 1 <= p <= X + 2:
+        if not partial:
             for slot in range(6):
                 PZ[slot, p, q, :] = pz[slot]
-        if p in kept:
+        if keep is not None:
             for i in range(3):
-                DZ[i, kept[p], q, :] = dz[i]
-        slope[p] = dz
-
-    def rates(p, r, slope):
+                DZ[i, keep, q, :] = dz[i]
+        slope.append(dz)
+
+    def rates(p, r, dz):
         q = slice(r, r + 8)
         m = PAD + r
         dx = [U[i, p + 1, m:m + 8, :] - U[i, p - 1, m:m + 8, :] for i in range(3)]
         dy = [U[i, p, m + 1:m + 9, :] - U[i, p, m - 1:m + 7, :] for i in range(3)]
-        dz = slope[p] if p in slope else [DZ[i, kept[p], q, :] for i in range(3)]
+        if not isinstance(dz, list):
+            dz = [DZ[i, dz, q, :] for i in range(3)]
         terms, mag = shear_terms(dx, dy, dz, 1.0)
         MAG[p, q, :] = mag
         for slot in range(6):
             ST[slot, p, q, :] = mag * terms[slot]
 
     def smooth(planes, r):
+        q = slice(r, r + 8)
+        for i in range(3):
+            for p in planes:
+                HU[i, p, PAD + r:PAD + r + 8, :] = 0.25 * (
+                    (ZS[i, p - 1, q, :] + ZS[i, p + 1, q, :]) + 2.0 * ZS[i, p, q, :]
+                )
+
+    def smooth_own(planes, r):
         q = slice(r, r + 8)
         for i in range(3):
             pair = {}
@@ -182,44 +258,35 @@
                         pair[s] = ZS[i, s, q, :] + ZS[i, s + 1, q, :]
                 HU[i, p, PAD + r:PAD + r + 8, :] = 0.25 * (pair[p - 1] + pair[p])
 
-    def stage_a(z_planes, planes):
-        for r in range(0, Y, 8):
-            slope = {}
-            for p in z_planes:
-                along_z(p, r, slope)
-            for p in planes:
-                rates(p, r, slope)
-            smooth(planes, r)
-        ghosts(HU, planes)
-
     def test_side(h, dx, dy, dz, px, sz):
         terms, mag = shear_terms(dx, dy, dz, 16.0)
         leonard = [px[slot] - h[i] * h[j] for slot, (i, j) in enumerate(pairs)]
         model = [sz[slot] - mag * terms[slot] for slot in range(6)]
         return contraction(leonard, model)
 
-    def stage_b(planes):
-        for r in range(0, Y, 8):
+    def stage_b(spots, at, first=0, last=Y):
+        for r in range(first, last, 8):
             q = slice(r, r + 8)
             m = PAD + r
             pair = {}
 
-            def x_sum(ref, slot, p):
-                for s in (p - 1, p):
+            def x_sum(ref, slot, k):
+                for s in (k - 1, k):
                     if (id(ref), slot, s) not in pair:
-                        pair[id(ref), slot, s] = ref[slot, s, q, :] + ref[slot, s + 1, q, :]
-                return pair[id(ref), slot, p - 1] + pair[id(ref), slot, p]
+                        pair[id(ref), slot, s] = ref[slot, at(s), q, :] + ref[slot, at(s + 1), q, :]
+                return pair[id(ref), slot, k - 1] + pair[id(ref), slot, k]
 
             total = None
-            for p in planes:
+            for k in spots:
+                p = at(k)
                 h = [HU[i, p, m:m + 8, :] for i in range(3)]
                 dx = [HU[i, p + 1, m:m + 8, :] - HU[i, p - 1, m:m + 8, :] for i in range(3)]
                 dy = [HU[i, p, m + 1:m + 9, :] - HU[i, p, m - 1:m + 7, :] for i in range(3)]
                 dz = [ahead(f) - behind(f) for f in h]
-                px = [x_sum(PZ, slot, p) for slot in range(6)]
+                px = [x_sum(PZ, slot, k) for slot in range(6)]
                 sz = []
                 for slot in range(6):
-                    sx = x_sum(ST, slot, p)
+                    sx = x_sum(ST, slot, k)
                     two = sx + behind(sx)
                     sz.append(two + ahead(two))
                 found = test_side(h, dx, dy, dz, px, sz)
@@ -231,19 +298,77 @@
     WD[...] = jnp.zeros_like(WD)
     own = range(2, X + 2)
     ghosts(U, own)
-    stage_a(own, range(3, X + 1))
-    stage_b(range(4, X))
-
-    for copy in beside:
-        copy.wait_recv()
-    corners = [send(8, GX, GL, (gx, zr)), send(9, GX, GR, (gx, zl))]
-
-    for copy in near:
-        copy.wait_recv()
-    ghosts(U, (1, X + 2))
-    stage_a((1, X + 2), (2, X + 1))
-    stage_b((3,))
-    stage_b((X,))
+    for r in range(0, Y, 8):
+        slope = []
+        for p in own:
+            along_z(p, r, slope, {2: 0, X + 1: 1}.get(p), False)
+        for p in own[1:-1]:
+            rates(p, r, slope[p - 2])
+        smooth_own(own[1:-1], r)
+    ghosts(HU, own[1:-1])
+    stage_b(own[2:-2], lambda k: k)
+
+    fast = 1 - lax.rem(gx, 2)
+
+    def arrive(side, part):
+        ext = side * (X + 3) + (1 - 2 * side) * parts[part][2]
+        halo_copy(part, side, ext, ext, (xl, gz)).wait_recv()
+
+    def boundary(side, near, far, first=0, last=Y):
+        def at(k):
+            return side * (X + 3) + (1 - 2 * side) * k
+
+        if near:
+            ghosts(U, [at(1)])
+        fresh = [at(2)] * near + [at(1)] * far
+        for r in range(first, last, 8):
+            slope = []
+            if near:
+                along_z(at(1), r, slope, None if far else 2 + side, False)
+            if far:
+                along_z(at(0), r, [], None, True)
+            if near:
+                rates(at(2), r, side)
+            if far:
+                rates(at(1), r, slope[0] if near else 2 + side)
+            smooth(fresh, r)
+        if near:
+            ghosts(HU, [at(2)])
+        stage_b([3] * near + [2] * far, at, first, last)
+
+    def strip_arrives(side):
+        send(side, EX.at[0], GX.at[side], (xl, gz)).wait_recv()
+
+    def forward(side):
+        return (
+            send(10 + side, GX.at[side], GL.at[side], (gx, zr)),
+            send(12 + side, GX.at[side], GR.at[side], (gx, zl)),
+        )
+
+    slow = 1 - fast
+    spread(range(0, 1))
+    strip_arrives(fast)
+    corners = [*forward(fast), *forward(slow)]
+    corners[0].start()
+
+    @pl.when(gz > 0)
+    def _():
+        corners[1].start()
+
+    for part in range(3):
+        arrive(fast, part)
+    boundary(fast, True, True)
+    strip_arrives(slow)
+    corners[2].start()
+
+    @pl.when(gz == 0)
+    def _():
+        pl.semaphore_wait(wrap_sem, 1)
+        edges[1].start()
+        corners[1].start()
+
+    corners[3].start()
+    spread(range(1, 2))
 
     y = lane - jnp.where(left, 0, Y)
     plus_by = jnp.where(y == 0, 2.0, jnp.where(y == Y - 1, 0.0, 1.0))
@@ -303,6 +428,10 @@
         WD[0] += total[0]
         WD[1] += total[1]
 
+    arrive(slow, 0)
+    boundary(slow, True, False)
+    spread(range(2, len(rounds)))
+
     for copy in edges:
         copy.wait_recv()
     cells = {p: [] for p in own}
@@ -313,16 +442,10 @@
             second = (jnp.where(left, zb, swap(rb)), jnp.where(left, swap(zb), rb))
             for odd in range(2):
                 for side in range(2):
-                    cells[2 + 2 * j + odd + side * half].append(join(odd, first[side], second[side]))
+                    x = partner(2 * j + odd) if side else 2 * j + odd
+                    cells[2 + x].append(join(odd, first[side], second[side]))
     window_a(cells, range(3, X + 1))
     window_b(range(4, X))
-
-    for copy in far:
-        copy.wait_recv()
-    ghosts(U, (0, X + 3))
-    stage_a((0, X + 3), (1, X + 2))
-    stage_b((2,))
-    stage_b((X + 1,))
 
     for copy in corners:
         copy.wait_recv()
@@ -336,6 +459,11 @@
     window_a(cells, (1, 2, X + 1, X + 2))
     window_b((2, 3, X, X + 1))
 
+    arrive(slow, 1)
+    boundary(slow, False, True, 0, deep)
+    arrive(slow, 2)
+    boundary(slow, False, True, deep, Y)
+
     take = (left & ((sub == 4) | (sub == 5))) | (~left & ((sub == 2) | (sub == 3)))
     numer = jnp.sum(jnp.where(take, WD[0], 0.0), axis=0, keepdims=True)
     denom = jnp.sum(jnp.where(take, WD[1], 0.0), axis=0, keepdims=True)
@@ -351,7 +479,11 @@
             device_id=peer, device_id_type=MESH,
         )
 
-    pl.semaphore_wait(row_sem, nx - 1)
+
+    @pl.when(gz < nz - 1)
+    def _():
+        pl.semaphore_wait(all_sem, 1)
+
     to_line(lambda peer: total_copy(peer).start(), count, anywhere)
 
     back = jnp.concatenate([WM[p] for p in own], axis=0)
@@ -363,7 +495,7 @@
         high_lane = pltpu.roll(BACK[Y:], (Z - 1 - 8 * x - 3) % Z, 1)
         mag = MAG[x + 2]
         mag_out[x] = jnp.where(spot == 0, low_lane, jnp.where(spot == Z - 1, high_lane, mag))
-    for copy in beside + edges + near + far + corners:
+    for copy in beside + edges + halo + corners:
         copy.wait_send()
     everyone = GOT.at[pl.ds(0, count - 1)]
     pltpu.make_async_copy(everyone, everyone, sum_recv).wait()
@@ -422,11 +554,13 @@
             pltpu.VMEM((2, 8, 2 * Y), f32),
             pltpu.VMEM((2 * Y, Z), f32),
             pltpu.VMEM((nx * nz, 1, 2 * Y), f32),
-            dma,
-            dma((10,)),
-            dma((10,)),
+            dma((3,)),
+            dma((14,)),
+            dma((14,)),
             dma,
             dma,
+            pltpu.SemaphoreType.REGULAR((len(knowledge_rounds(nx)),)),
+            pltpu.SemaphoreType.REGULAR,
             pltpu.SemaphoreType.REGULAR,
         ],
         compiler_params=pltpu.CompilerParams(collective_id=0, has_side_effects=True),

time: 18.9 us -> 18.6 us (0.984)
  Pallas kernels: 18.1 us -> 17.8 us
    pallas_call x1, Pallas kernels: 17.3 us -> 16.9 us  [on_device(): pl.pallas_call(functools.partial(kernel, axes, sizes), out_shape=(pltpu.V...]
where the time goes in v2:
time: 18.6 us; the launch traced here: 18.4 us
  Pallas kernels  17.8 us (96%)
  between operations  0.64 us (3%)
    pallas_call x1, Pallas kernels, on_device(): pl.pallas_call(functools.partial(kernel, axes, sizes), out_shape=(pltpu.V...  16.9 us
    pallas_call x1, Pallas kernels, on_device(): pl.pallas_call(functools.partial(finish, cells), out_shape=(jax.ShapeDtyp...  0.87 us

profile of v2, /device:TPU:0, one launch (start us, length us, event | category | flops | bytes accessed | tf_op | source)
XLA Modules:
  0.0 18.4 jit_solution(17117789938565166473)
XLA Ops:
  0.6 16.9 %shard_map.30 = (f32[1,128]{1,0:T(1,128)S(1)}, f32[8,64,128]{2,1,0:T(8,128)S(1)}) custom-call(f32[3,8,64,128]{3,2,1,0:T(8,128)} %vel.1), custom_call_target="tpu_custom_call" | custom-call | tf_op jit(solution)/shard_map/pallas_call | solution.py:527
  17.6 0.9 %shard_map.31 = (f32[64]{0:T(128)}, f32[8,64,128]{2,1,0:T(8,128)}) custom-call(f32[1,128]{1,0:T(1,128)S(1)} %get-tuple-element.4.sums, f32[8,64,128]{2,1,0:T(8,128)S(1)} %get-tuple-element.5.mag), custom_call_target="tpu_custom_call" | custom-call | tf_op jit(solution)/shard_map/pallas_call | solution.py:568
